TPU v7x, 128 devices: a whole 4x4x4 slice. The times are simulated.
128 devices in a mesh: dp: 8 (over x, core), crop: 4 (over y), tensor: 4 (over z).
Axes of the slice: x: 4, y: 4, z: 4, core: 2. Of those that a mesh axis runs over, the one named last changes fastest.
Arguments:
- hidden_a: bfloat16 [2048, 8192], P('crop', 'dp'), as said below
- hidden_b: bfloat16 [2048, 8192], P('crop', 'dp'), as said below
- weight: bfloat16 [8192, 8192], P('dp', 'tensor')
Outputs:
- weight_grad: float32 [8192, 8192], P(('dp', 'crop'), 'tensor')
Inputs may be any that keep to these rules, and one draw needn't show every extreme that they name: `hidden_a`: nonnegative entries. `hidden_b`: nonnegative entries.
All inputs are finite; a program needn't handle non-finite values.
Results may differ from a plain program's by a relative error of at most 0.0015.
Values may be sent and summed in bfloat16 or wider, within the bound.
A program may use at most 128 MiB of HBM per device.

v0:
```python
import jax
import jax.numpy as jnp
from jax import lax
from jax.sharding import PartitionSpec as P

epsilon = 0.0001


def sent_to_all(array, axis):
    peers = lax.axis_size(axis)
    return lax.all_to_all(
        jnp.broadcast_to(array[None], (peers, *array.shape)), axis, 0, 0, tiled=True
    )


def over_copies(array, axis):
    return sent_to_all(array, axis).sum(axis=0)


def body(hidden_a, hidden_b, weight):
    group_size = lax.axis_size(("dp", "crop"))
    data_count = lax.axis_size("dp")
    block_rows = hidden_a.shape[0]
    local_rows = block_rows // data_count
    total_rows = local_rows * group_size
    left_part = jnp.dot(hidden_a, weight, preferred_element_type=jnp.float32)
    right_part = jnp.dot(hidden_b, weight, preferred_element_type=jnp.float32)
    joined = lax.psum_scatter(
        jnp.stack([left_part, right_part], axis=1), "dp", scatter_dimension=0, tiled=True
    ).astype(jnp.bfloat16)
    stacked = jnp.stack([joined[:, 0, :], joined[:, 1, :]]).astype(jnp.float32)
    col_means = over_copies(jnp.sum(stacked, axis=1), ("dp", "crop")) / total_rows
    centered = stacked - col_means[:, None, :]
    spread = over_copies(jnp.sum(centered * centered, axis=1), ("dp", "crop"))
    deviation = jnp.sqrt(spread / (total_rows - 1.0) + epsilon)
    rounded = centered.astype(jnp.bfloat16)
    everyone = lax.all_gather(rounded, ("dp", "crop"), axis=1, tiled=True)
    gram = jnp.einsum("vrf,vbf->vrb", rounded, everyone, preferred_element_type=jnp.float32)
    gram = over_copies(gram, "tensor")
    gram_low = gram.astype(jnp.bfloat16)
    products = jnp.einsum("vrb,vbf->vrf", gram_low, everyone, preferred_element_type=jnp.float32)
    hinge_rate = jnp.where(deviation < 1.0, 25.0 / ((total_rows - 1.0) * deviation), 0.0)[
        :, None, :
    ]
    differ = stacked[0] - stacked[1]
    pull_term = jnp.stack([differ, -differ]) * (50.0 / total_rows)
    cov_scale = 4.0 / (total_rows - 1.0) ** 2
    row_grads = (
        pull_term - hinge_rate * centered + cov_scale * (products - centered * spread[:, None, :])
    )
    row_grads = row_grads.astype(jnp.bfloat16)
    block_grads = lax.all_gather(row_grads, "dp", axis=1, tiled=True)
    across = (((0,), (0,)), ((), ()))
    left_part = lax.dot_general(
        hidden_a, block_grads[0], across, preferred_element_type=jnp.float32
    )
    right_part = lax.dot_general(
        hidden_b, block_grads[1], across, preferred_element_type=jnp.float32
    )
    return lax.psum_scatter(left_part + right_part, "crop", scatter_dimension=0, tiled=True)


def solution(mesh):
    placed = (P("crop", "dp"), P("crop", "dp"), P("dp", "tensor"))
    return jax.shard_map(
        body, mesh=mesh, in_specs=placed, out_specs=P(("dp", "crop"), "tensor"), check_vma=False
    )
```

profile of v0, /device:TPU:1, one launch (start us, length us, event | category | flops | bytes accessed | tf_op | source)
XLA Modules:
  0.0 376.3 jit_solution(18045313686721249146)
XLA Ops:
  6.5 0.0 copy-start
  6.5 0.0 reduce-scatter.3.cloned.1.call-start
  6.5 0.0 copy-start.4
  6.5 5.0 %convolution_bitcast_fusion = f32[512,1,2048]{2,0,1:T(8,128)S(1)} fusion(bf16[512,1024]{1,0:T(8,128)(2,1)} %param.4, bf16[1024,2048]{1,0:T(8,128)(2,1)} %param.5), kind=kOutput, calls=%fused_computation.2 | convolution fusion | flops 2147483648 | bytes 9437184 | tf_op jit(solution)/shard_map/dot_general | solution.py:27
  11.5 0.0 copy-done
  11.5 0.0 copy-done.4
  11.6 2.4 convolution_bitcast_fusion.1
  13.9 3.8 %pad_maximum_fusion = f32[512,2,2048]{2,0,1:T(8,128)} fusion(f32[512,1,2048]{2,0,1:T(8,128)S(1)} %convolution_bitcast_fusion, f32[512,1,2048]{2,0,1:T(8,128)S(1)} %convolution_bitcast_fusion.1), kind=kLoop, calls=%fused_computation | loop fusion | flops 2097152 | bytes 16777216 | tf_op jit(solution)/shard_map/stack | solution.py:29
  17.7 0.0 reduce-scatter.3.cloned.1.call-update
  17.7 0.0 all-gather.3.cloned.1.call-start
  17.8 55.2 %reduce-scatter.3.cloned.1.call-done = f32[64,2,2048]{2,0,1:T(8,128)} async-done(((f32[512,2,2048]{2,0,1:T(8,128)}), f32[64,2,2048]{2,0,1:T(8,128)}) %reduce-scatter.3.cloned.1.call-update) | async-done | bytes 1048592 | tf_op jit(solution)/shard_map/reduce_scatter | solution.py:28
  73.0 1.3 convert_element_type.15
  74.3 0.1 convert_reduce_fusion
  74.4 0.2 broadcast_in_dim.9
  74.7 17.3 %all_to_all.15 = f32[32,2,2048]{2,1,0:T(2,128)S(1)} all-to-all(f32[32,2,2048]{2,1,0:T(2,128)S(1)} %broadcast_in_dim.9), channel_id=1, replica_groups=mesh['dp'=8,'crop'=4,'tensor'=4] {'dp','crop'}, dimensions={0} | all-to-all | bytes 1048576 | tf_op jit(solution)/shard_map/all_to_all | solution.py:11
  92.0 0.2 reduce_sum.46
  92.1 1.0 multiply_reduce_fusion
  93.1 0.0 all-gather.3.cloned.1.call-update
  93.1 1.0 broadcast_in_dim.10
  94.2 4.5 %all-to-all-start.1 = ((f32[32,2,2048]{2,1,0:T(2,128)}), f32[32,2,2048]{2,1,0:T(2,128)S(1)}, u32[]{:S(2)}, u32[]{:S(2)}) async-start(f32[32,2,2048]{2,1,0:T(2,128)} %broadcast_in_dim.10), calls=%async_computation.2 | async-start | bytes 1048576 | tf_op jit(solution)/shard_map/all_to_all | solution.py:11
  98.6 67.9 %all-gather.3.cloned.1.call-done = bf16[2,2048,2048]{2,1,0:T(8,128)(2,1)} async-done(((bf16[2,64,2048]{2,1,0:T(8,128)(2,1)}), bf16[2,2048,2048]{2,1,0:T(8,128)(2,1)}) %all-gather.3.cloned.1.call-update) | async-done | bytes 16777232 | tf_op jit(solution)/shard_map/all_gather | solution.py:37
  166.5 11.1 %fusion.8 = f32[2,64,2048]{2,1,0:T(8,128)S(1)} fusion(bf16[2,64,2048]{2,1,0:T(8,128)(2,1)} %get-tuple-element.8, bf16[2,2048,2048]{2,1,0:T(8,128)(2,1)} %all-gather.3.cloned.1.call-done), kind=kOutput, calls=%fused_computation.25 | convolution fusion | flops 1073741824 | bytes 18350080 | tf_op jit(solution)/shard_map/vrf,vbf->vrb/dot_general | solution.py:38
  177.6 0.0 all-to-all-done.1
  177.6 2.6 broadcast_in_dim.12
  180.2 4.8 %all-to-all-start.2 = ((f32[4,2,64,2048]{3,2,1,0:T(8,128)}), f32[4,2,64,2048]{3,2,1,0:T(8,128)}, u32[]{:S(2)}, u32[]{:S(2)}) async-start(f32[4,2,64,2048]{3,2,1,0:T(8,128)} %broadcast_in_dim.12), calls=%async_computation.3 | async-start | bytes 8388608 | tf_op jit(solution)/shard_map/all_to_all | solution.py:11
  185.0 0.2 all-gather.5.cloned.1.call-start
  185.3 0.1 fusion.6
  185.3 0.9 fusion.7
  186.2 0.2 reduce_sum.48
  186.4 0.0 copy-start.2
  186.5 47.3 %all-to-all-done.2 = f32[4,2,64,2048]{3,2,1,0:T(8,128)} async-done(((f32[4,2,64,2048]{3,2,1,0:T(8,128)}), f32[4,2,64,2048]{3,2,1,0:T(8,128)}, u32[]{:S(2)}, u32[]{:S(2)}) %all-to-all-start.2) | async-done | bytes 4194336 | tf_op jit(solution)/shard_map/all_to_all | solution.py:11
  233.7 2.6 reduce_sum.49
  236.3 0.0 copy-done.2
  236.4 9.8 %fusion.2 = bf16[2,64,2048]{2,1,0:T(8,128)(2,1)} fusion(bf16[2,2048,2048]{2,1,0:T(8,128)(2,1)} %all-gather.3.cloned.1.call-done, f32[1,64,2048]{2,1,0:T(8,128)S(1)} %get-tuple-element.5, f32[1,64,2048]{2,1,0:T(8,128)S(1)} %copy-done.2, f32[2,2048]{1,0:T(2,128)S(1)} %reduce_sum.48, bf16[2,64,2048]{2,1,0:T(8,128)(2,1)S(1)} %reduce_sum.49, ...), kind=kOutput, calls=%fused_computation.7 | convolution fusion | flops 1076887552 | bytes 19447808 | tf_op jit(solution)/shard_map/vrb,vbf->vrf/dot_general | solution.py:41
  246.1 0.0 all-gather.5.cloned.1.call-update
  246.1 0.0 copy-start.3
  246.2 0.0 reduce-scatter.5.cloned.1.call-start
  246.2 30.5 %all-gather.5.cloned.1.call-done = bf16[2,512,2048]{2,1,0:T(8,128)(2,1)} async-done(((bf16[2,64,2048]{2,1,0:T(8,128)(2,1)}), bf16[2,512,2048]{2,1,0:T(8,128)(2,1)}) %all-gather.5.cloned.1.call-update) | async-done | bytes 4194320 | tf_op jit(solution)/shard_map/all_gather | solution.py:52
  276.7 0.0 copy-start.1
  276.7 4.1 %fusion.3 = f32[2048,1024]{1,0:T(8,128)S(1)} fusion(bf16[512,1024]{1,0:T(8,128)(2,1)S(1)} %copy-done, bf16[2,512,2048]{2,1,0:T(8,128)(2,1)} %all-gather.5.cloned.1.call-done), kind=kOutput, calls=%fused_computation.10 | convolution fusion | flops 2147483648 | bytes 11534336 | tf_op jit(solution)/shard_map/dot_general | solution.py:54
  280.8 0.0 copy-done.3
  280.9 0.0 copy-done.1
  280.9 5.8 %add_bitcast_fusion = f32[1024,2048]{0,1:T(8,128)} fusion(f32[2048,1024]{1,0:T(8,128)S(1)} %fusion.3, bf16[512,1024]{1,0:T(8,128)(2,1)S(1)} %copy-done.3, bf16[2,512,2048]{2,1,0:T(8,128)(2,1)S(1)} %copy-done.1), kind=kOutput, calls=%fused_computation.1 | convolution fusion | flops 2149580800 | bytes 19922944 | tf_op jit(solution)/shard_map/dot_general | solution.py:57
  286.7 0.0 reduce-scatter.5.cloned.1.call-update
  286.7 80.2 %reduce-scatter.5.cloned.1.call-done = f32[256,2048]{0,1:T(8,128)} async-done(((f32[1024,2048]{0,1:T(8,128)}), f32[256,2048]{0,1:T(8,128)}) %reduce-scatter.5.cloned.1.call-update) | async-done | bytes 2097168 | tf_op jit(solution)/shard_map/reduce_scatter | solution.py:60
  366.9 2.9 copy.8
  (3 shorter events, 0.1 us)
Async XLA Ops:
  6.5 5.0 %copy-start = (bf16[512,1024]{1,0:T(8,128)(2,1)S(1)}, bf16[512,1024]{1,0:T(8,128)(2,1)}, u32[]{:S(2)}) copy-start(bf16[512,1024]{1,0:T(8,128)(2,1)} %param.3) | copy-start | bytes 3145732
  6.5 66.4 %reduce-scatter.3.cloned.1.call-start = ((), (), s32[]{:S(2)}) async-start(), calls=%async_computation.5 | async-start | bytes 9437184 | tf_op jit(solution)/shard_map/reduce_scatter | solution.py:28
  6.5 5.0 %copy-start.4 = (bf16[1024,2048]{1,0:T(8,128)(2,1)S(1)}, bf16[1024,2048]{1,0:T(8,128)(2,1)}, u32[]{:S(2)}) copy-start(bf16[1024,2048]{1,0:T(8,128)(2,1)} %param.5) | copy-start | bytes 12582916
  17.7 148.7 %all-gather.3.cloned.1.call-start = ((), (), s32[]{:S(2)}) async-start(), calls=%async_computation.6 | async-start | bytes 17301504 | tf_op jit(solution)/shard_map/all_gather | solution.py:37
  94.2 83.5 %all-to-all-start.1 = ((f32[32,2,2048]{2,1,0:T(2,128)}), f32[32,2,2048]{2,1,0:T(2,128)S(1)}, u32[]{:S(2)}, u32[]{:S(2)}) async-start(f32[32,2,2048]{2,1,0:T(2,128)} %broadcast_in_dim.10), calls=%async_computation.2 | async-start | bytes 1048576 | tf_op jit(solution)/shard_map/all_to_all | solution.py:11
  180.2 53.6 %all-to-all-start.2 = ((f32[4,2,64,2048]{3,2,1,0:T(8,128)}), f32[4,2,64,2048]{3,2,1,0:T(8,128)}, u32[]{:S(2)}, u32[]{:S(2)}) async-start(f32[4,2,64,2048]{3,2,1,0:T(8,128)} %broadcast_in_dim.12), calls=%async_computation.3 | async-start | bytes 8388608 | tf_op jit(solution)/shard_map/all_to_all | solution.py:11
  185.0 91.7 %all-gather.5.cloned.1.call-start = ((), (), s32[]{:S(2)}) async-start(), calls=%async_computation.7 | async-start | bytes 4718592 | tf_op jit(solution)/shard_map/all_gather | solution.py:52
  186.4 49.9 %copy-start.2 = (f32[1,64,2048]{2,1,0:T(8,128)S(1)}, f32[1,64,2048]{2,1,0:T(8,128)}, u32[]{:S(2)}) copy-start(f32[1,64,2048]{2,1,0:T(8,128)} %get-tuple-element.6) | copy-start | bytes 1572868
  246.1 34.7 %copy-start.3 = (bf16[512,1024]{1,0:T(8,128)(2,1)S(1)}, bf16[512,1024]{1,0:T(8,128)(2,1)}, u32[]{:S(2)}) copy-start(bf16[512,1024]{1,0:T(8,128)(2,1)} %param.4) | copy-start | bytes 3145732
  246.2 120.7 %reduce-scatter.5.cloned.1.call-start = ((), (), s32[]{:S(2)}) async-start(), calls=%async_computation.8 | async-start | bytes 10485760 | tf_op jit(solution)/shard_map/reduce_scatter | solution.py:60
  276.7 4.2 %copy-start.1 = (bf16[2,512,2048]{2,1,0:T(8,128)(2,1)S(1)}, bf16[2,512,2048]{2,1,0:T(8,128)(2,1)}, u32[]{:S(2)}) copy-start(bf16[2,512,2048]{2,1,0:T(8,128)(2,1)} %all-gather.5.cloned.1.call-done) | copy-start | bytes 12582916
Sparse Core Ops, SparseCore 0:
  17.9 55.0 reduce-scatter.2
  93.2 73.2 all-gather.2
  246.3 30.3 all-gather.4
  286.8 80.0 reduce-scatter.4
where the time goes:
time: 377 us; the launch traced here: 376 us
  waiting for transfers between devices  281 us (75%)
  matrix products  38.2 us (10%)
  blocking collectives  17.3 us (5%)
  between operations  13.3 us (4%)
  other arithmetic  10.1 us (3%)
  starting transfers between devices  9.61 us (3%)
  local copies, waits for them, and re-layouts  6.74 us (2%)
    reduce_scatter x1, waiting for transfers between devices, body(): lax.psum_scatter(left_part + right_part, 'crop', scatter_dimension=0, til...  80.2 us
    all_gather x1, waiting for transfers between devices, body(): everyone = lax.all_gather(rounded, ('dp', 'crop'), axis=1, tiled=True)  67.9 us
    reduce_scatter x1, waiting for transfers between devices, body(): lax.psum_scatter(jnp.stack([left_part, right_part], axis=1), 'dp', scatte...  55.2 us
    all_to_all x2, waiting for transfers between devices, sent_to_all(): lax.all_to_all(jnp.broadcast_to(array[None], (peers, *array.shape)), axis...  47.3 us
    all_gather x1, waiting for transfers between devices, body(): block_grads = lax.all_gather(row_grads, 'dp', axis=1, tiled=True)  30.5 us
    all_to_all x1, blocking collectives, sent_to_all(): lax.all_to_all(jnp.broadcast_to(array[None], (peers, *array.shape)), axis...  17.3 us
    dot_general x1, matrix products, body(): jnp.einsum('vrf,vbf->vrb', rounded, everyone, preferred_element_type=jnp....  11.1 us
    dot_general x1, matrix products, body(): jnp.einsum('vrb,vbf->vrf', gram_low, everyone, preferred_element_type=jnp...  9.76 us
  transfers between devices with their start and end apart: 6, of which 5 were waited for; matrix products, arithmetic and copies ran while one was open for 4% of the time, Pallas kernels for 0%

commit v1 on v0

v1 whole, which is shorter than its diff:
```python
import functools

import jax
import jax.numpy as jnp
from jax import lax
from jax.experimental import pallas as pl
from jax.experimental.pallas import tpu as pltpu
from jax.sharding import PartitionSpec as P

MESH = pl.DeviceIdType.MESH
BF, F32 = jnp.bfloat16, jnp.float32
NSEM = 144
EPS = 0.0001
FULL = slice(None)


def mm(a, b, dims=(((1,), (0,)), ((), ()))):
    return lax.dot_general(a, b, dims, preferred_element_type=F32)


def kernel(ha, hb, w, out, hc, wb, acc, s_far, s_raw, s_acc, r_far, r_raw, r_acc, zb, cb, hall,
           ht, mx, my, mu, dd, dsum, gf, gb, gr, gp, lt, orecv, send, recv, lsem):
    dp = lax.axis_index("dp")
    y = lax.axis_index("crop")
    t = lax.axis_index("tensor")
    x, c = lax.div(dp, 2), lax.rem(dp, 2)
    rows = 2048
    alpha = 50.0 / rows
    cov = 4.0 / (rows - 1.0) ** 2
    sign = jnp.where(c == 0, 1.0, -1.0).astype(F32)

    def turn(v, k):
        return lax.rem(v + k + 4, 4)

    def at_x(k):
        return (2 * turn(x, k) + c, y, t)

    def at_y(k):
        return (dp, turn(y, k), t)

    def at_t(k):
        return (dp, y, turn(t, k))

    partner = (2 * x + 1 - c, y, t)
    count = [0]
    started = []

    def remote(src, dst, dev, index=None):
        if index is None:
            index = count[0]
            count[0] += 1
        return pltpu.make_async_remote_copy(
            src_ref=src, dst_ref=dst, send_sem=send.at[index], recv_sem=recv.at[index],
            device_id=dev, device_id_type=MESH)

    def go(src, dst, dev):
        copy = remote(src, dst, dev)
        copy.start()
        started.append(copy)
        return copy

    def load(src, dst, i):
        return pltpu.make_async_copy(src, dst, lsem.at[i])

    load_w = [load(w.at[:, pl.ds(512 * j, 512)], wb.at[c, :, pl.ds(512 * j, 512)], j) for j in range(4)]
    load_h = load(ha, hc.at[c], 4)
    own = [load(h.at[:, pl.ds(256 * y, 256)], hall.at[v, c, y], 5 + v) for v, h in enumerate((ha, hb))]

    @pl.when(c == 0)
    def _():
        load(ha, hc.at[c], 4).start()

    @pl.when(c == 1)
    def _():
        load(hb, hc.at[c], 4).start()

    for copy in load_w + own:
        copy.start()

    barrier = pltpu.get_barrier_semaphore()
    peers = [partner] + [f(k) for f in (at_x, at_y, at_t) for k in (1, 2, 3)]
    for peer in peers:
        pl.semaphore_signal(barrier, inc=1, device_id=peer, device_id_type=MESH)
    pl.semaphore_wait(barrier, len(peers))

    h_index = count[0]
    count[0] += 1

    @pl.when(c == 0)
    def _():
        remote(hb, hc.at[c], partner, h_index).start()

    @pl.when(c == 1)
    def _():
        remote(ha, hc.at[c], partner, h_index).start()

    swap_h = remote(ha, hc.at[c], partner, h_index)
    started.append(swap_h)
    swap_w = [go(w.at[:, pl.ds(512 * j, 512)], wb.at[c, :, pl.ds(512 * j, 512)], partner) for j in range(4)]

    deal = []
    for k in (1, 3, 2):
        for v, h in enumerate((ha, hb)):
            deal.append((k, v, go(h.at[:, pl.ds(256 * turn(y, k), 256)], hall.at[v, c, y], at_y(k))))

    load_h.wait()
    swap_h.wait_recv()

    def way(j):
        return 1 if j % 2 == 0 else -1

    far, raw, summed = {}, {}, {}

    def relay(j):
        d = way(j)
        far[j].wait_recv()
        s_acc[j] = (acc[j, pl.ds(128 * turn(x, d), 128), :] + r_far[j].astype(F32)).astype(BF)
        summed[j] = go(s_acc.at[j], r_acc.at[j], at_x(d))

    for j in range(4):
        load_w[j].wait()
        swap_w[j].wait_recv()

        def half(n, _):
            cols = pl.ds(pl.multiple_of(512 * j + 256 * n, 256), 256)
            acc[j, :, pl.ds(pl.multiple_of(256 * n, 256), 256)] = (
                mm(hc[0], wb[0, :, cols]) + mm(hc[1], wb[1, :, cols]))
            return 0

        lax.fori_loop(0, 2, half, 0)
        d = way(j)
        s_far[j] = acc[j, pl.ds(128 * turn(x, 2), 128), :].astype(BF)
        s_raw[j] = acc[j, pl.ds(128 * turn(x, -d), 128), :].astype(BF)
        far[j] = go(s_far.at[j], r_far.at[j], at_x(d))
        raw[j] = go(s_raw.at[j], r_raw.at[j], at_x(-d))
        if j > 0:
            relay(j - 1)
    relay(3)

    block = 4 * y + x
    for j in range(4):
        raw[j].wait_recv()
        summed[j].wait_recv()
        cols = slice(512 * j, 512 * j + 512)
        z = (acc[j, pl.ds(128 * x, 128), :] + r_raw[j].astype(F32) + r_acc[j].astype(F32)).astype(BF)
        zb[block, :, cols] = z
        mx[x, :, cols] = jnp.sum(z.astype(F32), axis=0, keepdims=True)

    cols_of = (pl.ds(0, 1024), pl.ds(1024, 1024))

    class Ring:
        def __init__(self, axis, colour, offset):
            self.axis, self.colour, self.offset = axis, colour, offset
            self.to = at_x if axis == 0 else at_y
            self.right = go(self.piece(0), self.piece(0), self.to(1))
            self.left = go(self.piece(0), self.piece(0), self.to(-1))

        def index(self, k):
            if self.axis == 0:
                return 4 * turn(y, self.offset) + turn(x, k)
            return 4 * turn(y, k) + turn(x, self.offset)

        def piece(self, k, part=pl.ds(0, 128)):
            return zb.at[self.index(k), part, cols_of[self.colour]]

        def take(self):
            low, high = pl.ds(0, 64), pl.ds(64, 64)
            self.right.wait_recv()
            self.on_right = go(self.piece(-1, low), self.piece(-1, low), self.to(1))
            self.left.wait_recv()
            self.on_left = go(self.piece(1, high), self.piece(1, high), self.to(-1))

        def end(self):
            self.on_right.wait_recv()
            self.on_left.wait_recv()

    x_first = Ring(0, 0, 0)
    y_first = Ring(1, 1, 0)
    x_rings = {0: Ring(0, 1, 0)}
    y_rings = {0: Ring(1, 0, 0)}

    hops = [go(mx.at[x], mx.at[x], at_x(k)) for k in (1, 3, 2)]
    for hop in hops:
        hop.wait_recv()
    my[y] = mx[0] + mx[1] + mx[2] + mx[3]
    hops = [go(my.at[y], my.at[y], at_y(k)) for k in (1, 3, 2)]
    for hop in hops:
        hop.wait_recv()
    mu[...] = (my[0] + my[1] + my[2] + my[3]) * (1.0 / rows)
    dd[...] = jnp.zeros_like(dd)

    def center(index, colour):
        cols = slice(1024 * colour, 1024 * colour + 1024)
        cent = zb[index, :, cols].astype(F32) - mu[:, cols]
        dd[:, cols] += jnp.sum(cent * cent, axis=0, keepdims=True)
        cb[index, :, cols] = cent.astype(BF)

    def center_ring(ring, ks):
        for k in ks:
            center(ring.index(k), ring.colour)

    center(block, 0)
    center(block, 1)

    for v in range(2):
        own[v].wait()
        deal.append((0, v, None))
    handed = []
    for k, v, copy in sorted(deal, key=lambda item: (item[0] != 0)):
        if copy is not None:
            copy.wait_recv()
        slot = hall.at[v, c, turn(y, -k)]
        handed.append(go(slot, slot, partner))

    x_first.take()
    for k in (-1, 1):
        y_rings[k] = Ring(1, 0, k)
    y_first.take()
    for k in (-1, 1):
        x_rings[k] = Ring(0, 1, k)
    center_ring(x_first, (-1, 1))
    center_ring(y_first, (-1, 1))
    x_rings[0].take()
    y_rings[0].take()
    x_first.end()
    y_rings[2] = Ring(1, 0, 2)
    y_first.end()
    x_rings[2] = Ring(0, 1, 2)
    center_ring(x_first, (2,))
    center_ring(y_first, (2,))
    center_ring(x_rings[0], (-1, 1))
    center_ring(y_rings[0], (-1, 1))

    for copy in handed:
        copy.wait_recv()

    def flip(i, _):
        v, r = lax.div(i, 16), lax.rem(i, 16)
        k, yy = lax.div(r, 8), lax.div(lax.rem(r, 8), 2)
        part = lax.rem(r, 2)
        where = pl.multiple_of(512 * yy + 256 * part, 256)
        tile = hall[v, k, yy, pl.ds(pl.multiple_of(256 * part, 256), 256), :]
        ht[v, pl.ds(pl.multiple_of(256 * k, 256), 256), pl.ds(where, 256)] = tile.T
        return 0

    before = 0
    for k in (-1, 1, 2):
        x_rings[k].take()
        y_rings[k].take()
        before_ring = {-1: 0, 1: -1, 2: 1}[k]
        x_rings[before_ring].end()
        y_rings[before_ring].end()
        center_ring(x_rings[before_ring], (2,))
        center_ring(y_rings[before_ring], (2,))
        center_ring(x_rings[k], (-1, 1))
        center_ring(y_rings[k], (-1, 1))
        if k == -1:
            lax.fori_loop(0, 32, flip, 0)

            def add_up(i, _):
                part = pl.ds(pl.multiple_of(128 * i, 128), 128)
                diff = ht[0, part, :].astype(F32) - ht[1, part, :].astype(F32)
                dsum[part, :] = jnp.sum(diff, axis=1, keepdims=True)
                return 0

            lax.fori_loop(0, 4, add_up, 0)
    x_rings[2].end()
    y_rings[2].end()
    center_ring(x_rings[2], (2,))
    center_ring(y_rings[2], (2,))

    mine = cb[block]

    def pair(p, _):
        one = cb[lax.rem(block + 2 * p, 16)]
        two = cb[lax.rem(block + 2 * p + 1, 16)]
        res = mm(mine, jnp.concatenate([one, two], axis=0), (((1,), (1,)), ((), ())))
        at = pl.ds(pl.multiple_of(256 * p, 256), 256)
        gf[:, at] = res
        gb[:, at] = res.astype(BF)
        return 0

    lax.fori_loop(0, 4, pair, 0)
    last = mm(mine, cb[lax.rem(block + 8, 16)], (((1,), (1,)), ((), ())))
    gf[:, 1024:] = last
    gb[:, 1024:] = last.astype(BF)

    def strip(v):
        return pl.ds(pl.multiple_of(32 * v, 32), 32)

    hops = [go(gb.at[strip(turn(t, k)), :], gr.at[t], at_t(k)) for k in (1, 3, 2)]
    for hop in hops:
        hop.wait_recv()
    total = gf[strip(t), :]
    for k in (1, 2, 3):
        total = total + gr[turn(t, k)].astype(F32)
    gp[y, x, strip(t), :] = total.astype(BF)

    def part_of(n, i):
        return pl.ds(n * i, n)

    class Turn:
        def __init__(self, axis, colour, depth):
            self.axis = axis
            self.cols = pl.ds(384 * colour, 384)
            self.done = depth
            self.to = (at_x, at_y, at_t)[axis]
            self.right = go(self.piece(0, None), self.piece(0, None), self.to(1))
            self.left = go(self.piece(0, None), self.piece(0, None), self.to(-1))

        def piece(self, k, half):
            spots = [x, y, t]
            spots[self.axis] = turn(spots[self.axis], k)
            px, py, pt = spots
            ix = pl.ds(0, 4) if 0 in self.done else px
            iy = pl.ds(0, 4) if 1 in self.done else py
            it = pl.ds(0, 128) if 2 in self.done else strip(pt)
            if half is not None:
                if 1 in self.done:
                    iy = pl.ds(2 * half, 2)
                elif 0 in self.done:
                    ix = pl.ds(2 * half, 2)
                elif 2 in self.done:
                    it = pl.ds(64 * half, 64)
                else:
                    it = pl.ds(pl.multiple_of(32 * pt + 16 * half, 16), 16)
            return gp.at[iy, ix, it, self.cols]

        def take(self):
            self.right.wait_recv()
            self.on_right = go(self.piece(-1, 0), self.piece(-1, 0), self.to(1))
            self.left.wait_recv()
            self.on_left = go(self.piece(1, 1), self.piece(1, 1), self.to(-1))

        def end(self):
            self.on_right.wait_recv()
            self.on_left.wait_recv()

    orders = ((2, 1, 0), (0, 2, 1), (1, 0, 2))

    spread = dd[...]
    dev = jnp.sqrt(spread * (1.0 / (rows - 1.0)) + EPS)
    rate = jnp.where(dev < 1.0, 25.0 / ((rows - 1.0) * dev), 0.0) + cov * spread
    dd[...] = rate

    def plain(n, _):
        j, p = lax.div(n, 2), lax.rem(n, 2)
        cols = pl.ds(pl.multiple_of(256 * n, 256), 256)
        at = pl.ds(pl.multiple_of(256 * p, 256), 256)
        right = cb[:, :, cols].reshape(2048, 256)
        acc[j, :, at] = (sign * alpha) * dsum[...] * mu[:, cols] - mm(ht[c], right) * dd[:, cols]
        return 0

    cuts = (0, 2, 4, 8)
    for phase in range(3):
        turns = [Turn(order[phase], colour, order[:phase]) for colour, order in enumerate(orders)]
        lax.fori_loop(cuts[phase], cuts[phase + 1], plain, 0)
        for one in turns:
            one.take()
        for one in turns:
            one.end()

    for copy in started:
        copy.wait_send()
    started.clear()

    def spread_panel(b, _):
        by, bx = lax.div(b, 4), lax.rem(b, 4)
        here = pl.ds(pl.multiple_of(128 * b, 128), 128)
        for j in range(9):
            other = lax.rem(b + j, 16)
            tile = gp[by, bx, :, 128 * j:128 * j + 128]
            zb[b, :, pl.ds(pl.multiple_of(128 * other, 128), 128)] = tile
            if 0 < j < 8:
                zb[other, :, here] = tile.T
        return 0

    lax.fori_loop(0, 16, spread_panel, 0)

    def factor(n, _):
        cols = pl.ds(pl.multiple_of(256 * n, 256), 256)
        res = mm(ht[c], zb[:, :, cols].reshape(2048, 256))
        diff = ht[0, :, cols].astype(F32) - ht[1, :, cols].astype(F32)
        lt[:, cols] = (cov * res + (sign * alpha) * diff).astype(BF)
        return 0

    lax.fori_loop(0, 8, factor, 0)

    theirs = pl.ds(pl.multiple_of(256 * (1 - c), 256), 256)
    ours = pl.ds(pl.multiple_of(256 * c, 256), 256)

    def finish(which, j):
        def step(p, _):
            cols = pl.ds(pl.multiple_of(512 * j + 256 * p, 256), 256)
            at = pl.ds(pl.multiple_of(256 * p, 256), 256)
            acc[j, which, at] += mm(lt[which, :], cb[:, :, cols].reshape(2048, 256))
            return 0

        lax.fori_loop(0, 2, step, 0)

    give = []
    for j in range(4):
        finish(theirs, j)
        give.append(go(acc.at[j, theirs, :], orecv.at[j], partner))
    stores = []
    for j in range(4):
        finish(ours, j)
        give[j].wait_recv()
        orecv[j] += acc[j, ours, :]
        stores.append(load(orecv.at[j], out.at[:, pl.ds(512 * j, 512)], 7 + j))
        stores[j].start()
    for copy in started:
        copy.wait_send()
    for copy in stores:
        copy.wait()


def body(hidden_a, hidden_b, weight):
    anywhere = pl.BlockSpec(memory_space=pl.ANY)
    vm = pltpu.VMEM
    return pl.pallas_call(
        kernel,
        out_shape=jax.ShapeDtypeStruct((256, 2048), F32),
        in_specs=[anywhere] * 3,
        out_specs=anywhere,
        scratch_shapes=[
            vm((2, 512, 1024), BF), vm((2, 1024, 2048), BF), vm((4, 512, 512), F32),
            vm((4, 128, 512), BF), vm((4, 128, 512), BF), vm((4, 128, 512), BF),
            vm((4, 128, 512), BF), vm((4, 128, 512), BF), vm((4, 128, 512), BF),
            vm((16, 128, 2048), BF), vm((16, 128, 2048), BF), vm((2, 2, 4, 512, 256), BF),
            vm((2, 512, 2048), BF), vm((4, 1, 2048), F32), vm((4, 1, 2048), F32),
            vm((1, 2048), F32), vm((1, 2048), F32), vm((512, 1), F32),
            vm((128, 1152), F32), vm((128, 1152), BF), vm((4, 32, 1152), BF),
            vm((4, 4, 128, 1152), BF), vm((512, 2048), BF), vm((4, 256, 512), F32),
            pltpu.SemaphoreType.DMA((NSEM,)), pltpu.SemaphoreType.DMA((NSEM,)),
            pltpu.SemaphoreType.DMA((12,)),
        ],
        compiler_params=pltpu.CompilerParams(
            collective_id=0, has_side_effects=True, vmem_limit_bytes=67000000),
        name="vicreg_grad",
    )(hidden_a, hidden_b, weight)


def solution(mesh):
    placed = (P("crop", "dp"), P("crop", "dp"), P("dp", "tensor"))
    return jax.shard_map(
        body, mesh=mesh, in_specs=placed, out_specs=P(("dp", "crop"), "tensor"), check_vma=False
    )
```

time: 377 us -> 146 us (0.39)
  waiting for transfers between devices: 281 us -> 0 us
  Pallas kernels: 0 us -> 142 us
  matrix products: 38.2 us -> 0 us
  blocking collectives: 17.3 us -> 0 us
  between operations: 13.3 us -> 0.01 us
  other arithmetic: 10.1 us -> 0 us
  starting transfers between devices: 9.61 us -> 0 us
    pallas_call x0 -> x1, Pallas kernels: none -> 142 us  [body(): pl.pallas_call(kernel, out_shape=jax.ShapeDtypeStruct((256, 2048), F32),...]
    reduce_scatter x2 -> x0, waiting for transfers between devices: 135 us -> none  [the longest x1 80.2 us: body(): lax.psum_scatter(left_part + right_part, 'crop', scatter_dimension=0, til...]
    all_gather x2 -> x0, waiting for transfers between devices: 98.4 us -> none  [the longest x1 67.9 us: body(): everyone = lax.all_gather(rounded, ('dp', 'crop'), axis=1, tiled=True)]
    all_to_all x2 -> x0, waiting for transfers between devices: 47.3 us -> none  [sent_to_all(): lax.all_to_all(jnp.broadcast_to(array[None], (peers, *array.shape)), axis...]
    dot_general x6 -> x0, matrix products: 38.2 us -> none  [the longest x1 11.1 us: body(): jnp.einsum('vrf,vbf->vrb', rounded, everyone, preferred_element_type=jnp....]
    all_to_all x1 -> x0, blocking collectives: 17.3 us -> none  [sent_to_all(): lax.all_to_all(jnp.broadcast_to(array[None], (peers, *array.shape)), axis...]
    all_to_all x2 -> x0, starting transfers between devices: 9.31 us -> none  [sent_to_all(): lax.all_to_all(jnp.broadcast_to(array[None], (peers, *array.shape)), axis...]
    reduce_sum x5 -> x0, other arithmetic: 4 us -> none  [the longest x3 2.93 us: over_copies(): return sent_to_all(array, axis).sum(axis=0)]
  transfers between devices with their start and end apart: 6 -> 0, of which waited for: 5 -> 0; matrix products, arithmetic and copies ran while one was open for 4% -> 0% of each run, Pallas kernels for 0% -> 0%
where the time goes in v1:
time: 146 us; the launch traced here: 145 us
  Pallas kernels  142 us (97%)
  local copies, waits for them, and re-layouts  3.14 us (2%)
    pallas_call x1, Pallas kernels, body(): pl.pallas_call(kernel, out_shape=jax.ShapeDtypeStruct((256, 2048), F32),...  142 us
    unnamed x1, local copies, waits for them, and re-layouts  3.14 us

profile of v1, /device:TPU:1, one launch (start us, length us, event | category | flops | bytes accessed | tf_op | source)
XLA Modules:
  0.0 144.7 jit_solution(1048016644487952590)
XLA Ops:
  0.0 141.5 %vicreg_grad.1 = f32[256,2048]{1,0:T(8,128)} custom-call(bf16[512,1024]{1,0:T(8,128)(2,1)} %ha.1, bf16[512,1024]{1,0:T(8,128)(2,1)} %hb.1, bf16[1024,2048]{1,0:T(8,128)(2,1)} %w.1), custom_call_target="tpu_custom_call" | custom-call | tf_op jit(solution)/shard_map/vicreg_grad/pallas_call | solution.py:421
  141.5 3.1 %copy.5 = f32[256,2048]{1,0:T(8,128)} copy(f32[256,2048]{1,0:T(8,128)} %vicreg_grad.1) | data formatting | bytes 4194304

commit v2 on v1

--- a/solution.py
+++ b/solution.py
@@ -9,7 +9,7 @@
 
 MESH = pl.DeviceIdType.MESH
 BF, F32 = jnp.bfloat16, jnp.float32
-NSEM = 144
+NSEM = 208
 EPS = 0.0001
 FULL = slice(None)
 
@@ -98,10 +98,13 @@
     started.append(swap_h)
     swap_w = [go(w.at[:, pl.ds(512 * j, 512)], wb.at[c, :, pl.ds(512 * j, 512)], partner) for j in range(4)]
 
+    def quarter(v):
+        return pl.ds(pl.multiple_of(128 * v, 128), 128)
+
     deal = []
     for k in (1, 3, 2):
         for v, h in enumerate((ha, hb)):
-            deal.append((k, v, go(h.at[:, pl.ds(256 * turn(y, k), 256)], hall.at[v, c, y], at_y(k))))
+            deal.append((k, v, go(h.at[quarter(t), pl.ds(256 * turn(y, k), 256)], hall.at[v, c, y, quarter(t)], at_y(k))))
 
     load_h.wait()
     swap_h.wait_recv()
@@ -202,15 +205,32 @@
     center(block, 0)
     center(block, 1)
 
+    class Rows:
+        def __init__(self, k, v):
+            self.slot = hall.at[v, c, turn(y, -k)]
+            mine = self.slot.at[quarter(t)]
+            self.right, self.left = go(mine, mine, at_t(1)), go(mine, mine, at_t(-1))
+
+        def take(self):
+            self.right.wait_recv()
+            piece = self.slot.at[pl.ds(pl.multiple_of(128 * turn(t, -1), 128), 64)]
+            self.on_right = go(piece, piece, at_t(1))
+            self.left.wait_recv()
+            piece = self.slot.at[pl.ds(pl.multiple_of(128 * turn(t, 1) + 64, 64), 64)]
+            self.on_left = go(piece, piece, at_t(-1))
+
+        def end(self):
+            self.on_right.wait_recv()
+            self.on_left.wait_recv()
+
+    handed = []
     for v in range(2):
         own[v].wait()
-        deal.append((0, v, None))
-    handed = []
-    for k, v, copy in sorted(deal, key=lambda item: (item[0] != 0)):
-        if copy is not None:
-            copy.wait_recv()
-        slot = hall.at[v, c, turn(y, -k)]
-        handed.append(go(slot, slot, partner))
+        handed.append(go(hall.at[v, c, y], hall.at[v, c, y], partner))
+    spans = []
+    for k, v, copy in deal:
+        copy.wait_recv()
+        spans.append(Rows(k, v))
 
     x_first.take()
     for k in (-1, 1):
@@ -220,6 +240,8 @@
         x_rings[k] = Ring(0, 1, k)
     center_ring(x_first, (-1, 1))
     center_ring(y_first, (-1, 1))
+    for span in spans:
+        span.take()
     x_rings[0].take()
     y_rings[0].take()
     x_first.end()
@@ -231,8 +253,9 @@
     center_ring(x_rings[0], (-1, 1))
     center_ring(y_rings[0], (-1, 1))
 
-    for copy in handed:
-        copy.wait_recv()
+    for span in spans:
+        span.end()
+        handed.append(go(span.slot, span.slot, partner))
 
     def flip(i, _):
         v, r = lax.div(i, 16), lax.rem(i, 16)
@@ -243,7 +266,6 @@
         ht[v, pl.ds(pl.multiple_of(256 * k, 256), 256), pl.ds(where, 256)] = tile.T
         return 0
 
-    before = 0
     for k in (-1, 1, 2):
         x_rings[k].take()
         y_rings[k].take()
@@ -255,6 +277,8 @@
         center_ring(x_rings[k], (-1, 1))
         center_ring(y_rings[k], (-1, 1))
         if k == -1:
+            for copy in handed:
+                copy.wait_recv()
             lax.fori_loop(0, 32, flip, 0)
 
             def add_up(i, _):
@@ -296,40 +320,32 @@
         total = total + gr[turn(t, k)].astype(F32)
     gp[y, x, strip(t), :] = total.astype(BF)
 
-    def part_of(n, i):
-        return pl.ds(n * i, n)
-
     class Turn:
-        def __init__(self, axis, colour, depth):
-            self.axis = axis
+        def __init__(self, axis, colour, done, fixed=None, offset=0):
+            self.axis, self.done, self.fixed, self.offset = axis, done, fixed, offset
             self.cols = pl.ds(384 * colour, 384)
-            self.done = depth
             self.to = (at_x, at_y, at_t)[axis]
-            self.right = go(self.piece(0, None), self.piece(0, None), self.to(1))
-            self.left = go(self.piece(0, None), self.piece(0, None), self.to(-1))
-
-        def piece(self, k, half):
+            self.sent = [go(self.piece(0), self.piece(0), self.to(k)) for k in ((1, -1) if done else (1, -1, 2))]
+
+        def piece(self, k, half=None):
             spots = [x, y, t]
+            if self.fixed is not None:
+                spots[self.fixed] = turn(spots[self.fixed], self.offset)
             spots[self.axis] = turn(spots[self.axis], k)
-            px, py, pt = spots
-            ix = pl.ds(0, 4) if 0 in self.done else px
-            iy = pl.ds(0, 4) if 1 in self.done else py
-            it = pl.ds(0, 128) if 2 in self.done else strip(pt)
-            if half is not None:
-                if 1 in self.done:
-                    iy = pl.ds(2 * half, 2)
-                elif 0 in self.done:
-                    ix = pl.ds(2 * half, 2)
-                elif 2 in self.done:
-                    it = pl.ds(64 * half, 64)
-                else:
-                    it = pl.ds(pl.multiple_of(32 * pt + 16 * half, 16), 16)
+            ix, iy, it = spots[0], spots[1], strip(spots[2])
+            if half is None:
+                whole = {0: pl.ds(0, 4), 1: pl.ds(0, 4), 2: pl.ds(0, 128)}
+            else:
+                whole = {0: pl.ds(2 * half, 2), 1: pl.ds(2 * half, 2), 2: pl.ds(64 * half, 64)}
+            ix = whole[0] if self.done == 0 + 1 else ix
+            iy = whole[1] if self.done == 1 + 1 else iy
+            it = whole[2] if self.done == 2 + 1 else it
             return gp.at[iy, ix, it, self.cols]
 
         def take(self):
-            self.right.wait_recv()
+            self.sent[0].wait_recv()
             self.on_right = go(self.piece(-1, 0), self.piece(-1, 0), self.to(1))
-            self.left.wait_recv()
+            self.sent[1].wait_recv()
             self.on_left = go(self.piece(1, 1), self.piece(1, 1), self.to(-1))
 
         def end(self):
@@ -351,14 +367,41 @@
         acc[j, :, at] = (sign * alpha) * dsum[...] * mu[:, cols] - mm(ht[c], right) * dd[:, cols]
         return 0
 
-    cuts = (0, 2, 4, 8)
-    for phase in range(3):
-        turns = [Turn(order[phase], colour, order[:phase]) for colour, order in enumerate(orders)]
-        lax.fori_loop(cuts[phase], cuts[phase + 1], plain, 0)
+    firsts = [Turn(a, i, 0) for i, (a, b, d) in enumerate(orders)]
+    lax.fori_loop(0, 2, plain, 0)
+    for first in firsts:
+        for copy in first.sent:
+            copy.wait_recv()
+    seconds = [Turn(b, i, a + 1) for i, (a, b, d) in enumerate(orders)]
+
+    def third(offset):
+        return [Turn(d, i, a + 1, b, offset) for i, (a, b, d) in enumerate(orders)]
+
+    def take(turns):
         for one in turns:
             one.take()
+
+    def end(turns):
         for one in turns:
             one.end()
+
+    thirds = {0: third(0)}
+    lax.fori_loop(2, 4, plain, 0)
+    take(seconds)
+    thirds[-1] = third(-1)
+    thirds[1] = third(1)
+    take(thirds[0])
+    lax.fori_loop(4, 6, plain, 0)
+    end(seconds)
+    thirds[2] = third(2)
+    lax.fori_loop(6, 7, plain, 0)
+    take(thirds[-1])
+    end(thirds[0])
+    take(thirds[1])
+    lax.fori_loop(7, 8, plain, 0)
+    take(thirds[2])
+    for offset in (-1, 1, 2):
+        end(thirds[offset])
 
     for copy in started:
         copy.wait_send()

time: 146 us -> 143 us (0.979)
  Pallas kernels: 142 us -> 138 us
    pallas_call x1, Pallas kernels: 142 us -> 138 us  [body(): pl.pallas_call(kernel, out_shape=jax.ShapeDtypeStruct((256, 2048), F32),...]
where the time goes in v2:
time: 143 us; the launch traced here: 142 us
  Pallas kernels  138 us (97%)
  local copies, waits for them, and re-layouts  3.14 us (2%)
    pallas_call x1, Pallas kernels, body(): pl.pallas_call(kernel, out_shape=jax.ShapeDtypeStruct((256, 2048), F32),...  138 us
    unnamed x1, local copies, waits for them, and re-layouts  3.14 us

profile of v2, /device:TPU:1, one launch (start us, length us, event | category | flops | bytes accessed | tf_op | source)
XLA Modules:
  0.0 141.5 jit_solution(17420758420596481293)
XLA Ops:
  0.0 138.4 %vicreg_grad.1 = f32[256,2048]{1,0:T(8,128)} custom-call(bf16[512,1024]{1,0:T(8,128)(2,1)} %ha.1, bf16[512,1024]{1,0:T(8,128)(2,1)} %hb.1, bf16[1024,2048]{1,0:T(8,128)(2,1)} %w.1), custom_call_target="tpu_custom_call" | custom-call | tf_op jit(solution)/shard_map/vicreg_grad/pallas_call | solution.py:464
  138.4 3.1 %copy.5 = f32[256,2048]{1,0:T(8,128)} copy(f32[256,2048]{1,0:T(8,128)} %vicreg_grad.1) | data formatting | bytes 4194304

commit v3 on v2

--- a/solution.py
+++ b/solution.py
@@ -10,6 +10,7 @@
 MESH = pl.DeviceIdType.MESH
 BF, F32 = jnp.bfloat16, jnp.float32
 NSEM = 208
+VMEM = 58 * 1024 * 1024
 EPS = 0.0001
 FULL = slice(None)
 
@@ -18,8 +19,8 @@
     return lax.dot_general(a, b, dims, preferred_element_type=F32)
 
 
-def kernel(ha, hb, w, out, hc, wb, acc, s_far, s_raw, s_acc, r_far, r_raw, r_acc, zb, cb, hall,
-           ht, mx, my, mu, dd, dsum, gf, gb, gr, gp, lt, orecv, send, recv, lsem):
+def kernel(ha, hb, w, kept, out, hc, wb, acc, s_part, r_part, s_far, s_raw, s_acc, r_far, r_raw, r_acc, zb, cb, hall,
+           ht, mx, my, mu, dd, dsum, gf, gb, gr, gp, lt, send, recv, lsem):
     dp = lax.axis_index("dp")
     y = lax.axis_index("crop")
     t = lax.axis_index("tensor")
@@ -62,41 +63,60 @@
     def load(src, dst, i):
         return pltpu.make_async_copy(src, dst, lsem.at[i])
 
-    load_w = [load(w.at[:, pl.ds(512 * j, 512)], wb.at[c, :, pl.ds(512 * j, 512)], j) for j in range(4)]
-    load_h = load(ha, hc.at[c], 4)
-    own = [load(h.at[:, pl.ds(256 * y, 256)], hall.at[v, c, y], 5 + v) for v, h in enumerate((ha, hb))]
-
-    @pl.when(c == 0)
-    def _():
-        load(ha, hc.at[c], 4).start()
-
-    @pl.when(c == 1)
-    def _():
-        load(hb, hc.at[c], 4).start()
-
-    for copy in load_w + own:
+    load_h = [load(h, hc.at[v], 4 + v) for v, h in enumerate((ha, hb))]
+    load_w = [load(w.at[:, pl.ds(512 * j, 512)], wb.at[:, pl.ds(512 * j, 512)], j) for j in range(4)]
+    own = [load(h.at[:, pl.ds(256 * y, 256)], hall.at[v, c, y], 6 + v) for v, h in enumerate((ha, hb))]
+    for copy in load_h + load_w + own:
         copy.start()
 
     barrier = pltpu.get_barrier_semaphore()
     peers = [partner] + [f(k) for f in (at_x, at_y, at_t) for k in (1, 2, 3)]
     for peer in peers:
         pl.semaphore_signal(barrier, inc=1, device_id=peer, device_id_type=MESH)
+
+    def way(j):
+        return 1 if j % 2 == 0 else -1
+
+    far, raw, summed = {}, {}, {}
+
+    def rows_of(j, k):
+        at = pl.ds(pl.multiple_of(128 * turn(x, k), 128), 128)
+        return acc[j, at, :] + r_part[j, at, :].astype(F32)
+
+    def join(j):
+        d = way(j)
+        part[j].wait_recv()
+        s_far[j] = rows_of(j, 2).astype(BF)
+        s_raw[j] = rows_of(j, -d).astype(BF)
+        far[j] = go(s_far.at[j], r_far.at[j], at_x(d))
+
+    def relay(j):
+        d = way(j)
+        far[j].wait_recv()
+        s_acc[j] = (rows_of(j, d) + r_far[j].astype(F32)).astype(BF)
+        summed[j] = go(s_acc.at[j], r_acc.at[j], at_x(d))
+
+    part = []
+
+    def theirs_of(j):
+        load_w[j].wait()
+        s_part[j] = mm(hc[1 - c], wb[:, 512 * j:512 * j + 512]).astype(BF)
+
+    def give_part(j):
+        part.append(go(s_part.at[j], r_part.at[j], partner))
+
+    def ours_of(j):
+        acc[j] = mm(hc[c], wb[:, 512 * j:512 * j + 512])
+
+    for copy in load_h:
+        copy.wait()
+    theirs_of(0)
     pl.semaphore_wait(barrier, len(peers))
-
-    h_index = count[0]
-    count[0] += 1
-
-    @pl.when(c == 0)
-    def _():
-        remote(hb, hc.at[c], partner, h_index).start()
-
-    @pl.when(c == 1)
-    def _():
-        remote(ha, hc.at[c], partner, h_index).start()
-
-    swap_h = remote(ha, hc.at[c], partner, h_index)
-    started.append(swap_h)
-    swap_w = [go(w.at[:, pl.ds(512 * j, 512)], wb.at[c, :, pl.ds(512 * j, 512)], partner) for j in range(4)]
+    give_part(0)
+    theirs_of(1)
+    give_part(1)
+    ours_of(0)
+    join(0)
 
     def quarter(v):
         return pl.ds(pl.multiple_of(128 * v, 128), 128)
@@ -106,50 +126,35 @@
         for v, h in enumerate((ha, hb)):
             deal.append((k, v, go(h.at[quarter(t), pl.ds(256 * turn(y, k), 256)], hall.at[v, c, y, quarter(t)], at_y(k))))
 
-    load_h.wait()
-    swap_h.wait_recv()
-
-    def way(j):
-        return 1 if j % 2 == 0 else -1
-
-    far, raw, summed = {}, {}, {}
-
-    def relay(j):
-        d = way(j)
-        far[j].wait_recv()
-        s_acc[j] = (acc[j, pl.ds(128 * turn(x, d), 128), :] + r_far[j].astype(F32)).astype(BF)
-        summed[j] = go(s_acc.at[j], r_acc.at[j], at_x(d))
-
+    for j in (1, 2, 3):
+        if j < 3:
+            theirs_of(j + 1)
+            give_part(j + 1)
+        ours_of(j)
+        join(j)
+
+    def send_raw(j):
+        raw[j] = go(s_raw.at[j], r_raw.at[j], at_x(-way(j)))
+
+    send_raw(0)
+    send_raw(1)
     for j in range(4):
-        load_w[j].wait()
-        swap_w[j].wait_recv()
-
-        def half(n, _):
-            cols = pl.ds(pl.multiple_of(512 * j + 256 * n, 256), 256)
-            acc[j, :, pl.ds(pl.multiple_of(256 * n, 256), 256)] = (
-                mm(hc[0], wb[0, :, cols]) + mm(hc[1], wb[1, :, cols]))
-            return 0
-
-        lax.fori_loop(0, 2, half, 0)
-        d = way(j)
-        s_far[j] = acc[j, pl.ds(128 * turn(x, 2), 128), :].astype(BF)
-        s_raw[j] = acc[j, pl.ds(128 * turn(x, -d), 128), :].astype(BF)
-        far[j] = go(s_far.at[j], r_far.at[j], at_x(d))
-        raw[j] = go(s_raw.at[j], r_raw.at[j], at_x(-d))
-        if j > 0:
-            relay(j - 1)
-    relay(3)
+        relay(j)
+    send_raw(2)
+    send_raw(3)
 
     block = 4 * y + x
-    for j in range(4):
+
+    def settle(j):
         raw[j].wait_recv()
         summed[j].wait_recv()
         cols = slice(512 * j, 512 * j + 512)
-        z = (acc[j, pl.ds(128 * x, 128), :] + r_raw[j].astype(F32) + r_acc[j].astype(F32)).astype(BF)
+        z = (rows_of(j, 0) + r_raw[j].astype(F32) + r_acc[j].astype(F32)).astype(BF)
         zb[block, :, cols] = z
         mx[x, :, cols] = jnp.sum(z.astype(F32), axis=0, keepdims=True)
 
-    cols_of = (pl.ds(0, 1024), pl.ds(1024, 1024))
+    split = 896
+    cols_of = (pl.ds(0, split), pl.ds(split, 2048 - split))
 
     class Ring:
         def __init__(self, axis, colour, offset):
@@ -176,34 +181,6 @@
         def end(self):
             self.on_right.wait_recv()
             self.on_left.wait_recv()
-
-    x_first = Ring(0, 0, 0)
-    y_first = Ring(1, 1, 0)
-    x_rings = {0: Ring(0, 1, 0)}
-    y_rings = {0: Ring(1, 0, 0)}
-
-    hops = [go(mx.at[x], mx.at[x], at_x(k)) for k in (1, 3, 2)]
-    for hop in hops:
-        hop.wait_recv()
-    my[y] = mx[0] + mx[1] + mx[2] + mx[3]
-    hops = [go(my.at[y], my.at[y], at_y(k)) for k in (1, 3, 2)]
-    for hop in hops:
-        hop.wait_recv()
-    mu[...] = (my[0] + my[1] + my[2] + my[3]) * (1.0 / rows)
-    dd[...] = jnp.zeros_like(dd)
-
-    def center(index, colour):
-        cols = slice(1024 * colour, 1024 * colour + 1024)
-        cent = zb[index, :, cols].astype(F32) - mu[:, cols]
-        dd[:, cols] += jnp.sum(cent * cent, axis=0, keepdims=True)
-        cb[index, :, cols] = cent.astype(BF)
-
-    def center_ring(ring, ks):
-        for k in ks:
-            center(ring.index(k), ring.colour)
-
-    center(block, 0)
-    center(block, 1)
 
     class Rows:
         def __init__(self, k, v):
@@ -232,30 +209,59 @@
         copy.wait_recv()
         spans.append(Rows(k, v))
 
+    settle(0)
+    settle(1)
+    y_first = Ring(1, 0, 0)
+    settle(2)
+    settle(3)
+    hops = [go(mx.at[x], mx.at[x], at_x(k)) for k in (1, 3, 2)]
+    x_first = Ring(0, 1, 0)
+    y_rings = {0: Ring(1, 1, 0)}
+    x_rings = {0: Ring(0, 0, 0)}
+    for hop in hops:
+        hop.wait_recv()
+    my[y] = mx[0] + mx[1] + mx[2] + mx[3]
+    hops = [go(my.at[y], my.at[y], at_y(k)) for k in (1, 3, 2)]
+    y_first.take()
+    for k in (-1, 1):
+        x_rings[k] = Ring(0, 0, k)
+    for span in spans:
+        span.take()
     x_first.take()
     for k in (-1, 1):
-        y_rings[k] = Ring(1, 0, k)
-    y_first.take()
-    for k in (-1, 1):
-        x_rings[k] = Ring(0, 1, k)
-    center_ring(x_first, (-1, 1))
-    center_ring(y_first, (-1, 1))
-    for span in spans:
-        span.take()
-    x_rings[0].take()
-    y_rings[0].take()
-    x_first.end()
-    y_rings[2] = Ring(1, 0, 2)
-    y_first.end()
-    x_rings[2] = Ring(0, 1, 2)
-    center_ring(x_first, (2,))
-    center_ring(y_first, (2,))
-    center_ring(x_rings[0], (-1, 1))
-    center_ring(y_rings[0], (-1, 1))
-
+        y_rings[k] = Ring(1, 1, k)
     for span in spans:
         span.end()
         handed.append(go(span.slot, span.slot, partner))
+    for hop in hops:
+        hop.wait_recv()
+    mu[...] = (my[0] + my[1] + my[2] + my[3]) * (1.0 / rows)
+    dd[...] = jnp.zeros_like(dd)
+
+    def center(index, colour):
+        cols = slice(split * colour, 2048 if colour else split)
+        cent = zb[index, :, cols].astype(F32) - mu[:, cols]
+        dd[:, cols] += jnp.sum(cent * cent, axis=0, keepdims=True)
+        cb[index, :, cols] = cent.astype(BF)
+
+    def center_ring(ring, ks):
+        for k in ks:
+            center(ring.index(k), ring.colour)
+
+    center(block, 0)
+    center(block, 1)
+    center_ring(y_first, (-1, 1))
+    center_ring(x_first, (-1, 1))
+    x_rings[0].take()
+    y_rings[0].take()
+    y_first.end()
+    x_rings[2] = Ring(0, 0, 2)
+    x_first.end()
+    y_rings[2] = Ring(1, 1, 2)
+    center_ring(y_first, (2,))
+    center_ring(x_first, (2,))
+    center_ring(x_rings[0], (-1, 1))
+    center_ring(y_rings[0], (-1, 1))
 
     def flip(i, _):
         v, r = lax.div(i, 16), lax.rem(i, 16)
@@ -279,7 +285,10 @@
         if k == -1:
             for copy in handed:
                 copy.wait_recv()
-            lax.fori_loop(0, 32, flip, 0)
+            lax.fori_loop(0, 16, flip, 0)
+        if k == 1:
+            lax.fori_loop(16, 32, flip, 0)
+        if k == 2:
 
             def add_up(i, _):
                 part = pl.ds(pl.multiple_of(128 * i, 128), 128)
@@ -295,30 +304,17 @@
 
     mine = cb[block]
 
-    def pair(p, _):
-        one = cb[lax.rem(block + 2 * p, 16)]
-        two = cb[lax.rem(block + 2 * p + 1, 16)]
-        res = mm(mine, jnp.concatenate([one, two], axis=0), (((1,), (1,)), ((), ())))
-        at = pl.ds(pl.multiple_of(256 * p, 256), 256)
-        gf[:, at] = res
-        gb[:, at] = res.astype(BF)
-        return 0
-
-    lax.fori_loop(0, 4, pair, 0)
-    last = mm(mine, cb[lax.rem(block + 8, 16)], (((1,), (1,)), ((), ())))
-    gf[:, 1024:] = last
-    gb[:, 1024:] = last.astype(BF)
-
     def strip(v):
         return pl.ds(pl.multiple_of(32 * v, 32), 32)
 
-    hops = [go(gb.at[strip(turn(t, k)), :], gr.at[t], at_t(k)) for k in (1, 3, 2)]
-    for hop in hops:
-        hop.wait_recv()
-    total = gf[strip(t), :]
-    for k in (1, 2, 3):
-        total = total + gr[turn(t, k)].astype(F32)
-    gp[y, x, strip(t), :] = total.astype(BF)
+    sums = []
+    for i in range(3):
+        cols = pl.ds(384 * i, 384)
+        right = jnp.concatenate([cb[lax.rem(block + 3 * i + q, 16)] for q in range(3)], axis=0)
+        res = mm(mine, right, (((1,), (1,)), ((), ())))
+        gf[:, cols] = res
+        gb[:, cols] = res.astype(BF)
+        sums.append([go(gb.at[strip(turn(t, k)), cols], gr.at[t, :, cols], at_t(k)) for k in (1, 3, 2)])
 
     class Turn:
         def __init__(self, axis, colour, done, fixed=None, offset=0):
@@ -354,6 +350,17 @@
 
     orders = ((2, 1, 0), (0, 2, 1), (1, 0, 2))
 
+    firsts = []
+    for i, order in enumerate(orders):
+        cols = pl.ds(384 * i, 384)
+        for hop in sums[i]:
+            hop.wait_recv()
+        total = gf[strip(t), cols]
+        for k in (1, 2, 3):
+            total = total + gr[turn(t, k), :, cols].astype(F32)
+        gp[y, x, strip(t), cols] = total.astype(BF)
+        firsts.append(Turn(order[0], i, 0))
+
     spread = dd[...]
     dev = jnp.sqrt(spread * (1.0 / (rows - 1.0)) + EPS)
     rate = jnp.where(dev < 1.0, 25.0 / ((rows - 1.0) * dev), 0.0) + cov * spread
@@ -367,7 +374,6 @@
         acc[j, :, at] = (sign * alpha) * dsum[...] * mu[:, cols] - mm(ht[c], right) * dd[:, cols]
         return 0
 
-    firsts = [Turn(a, i, 0) for i, (a, b, d) in enumerate(orders)]
     lax.fori_loop(0, 2, plain, 0)
     for first in firsts:
         for copy in first.sent:
@@ -421,37 +427,30 @@
     lax.fori_loop(0, 16, spread_panel, 0)
 
     def factor(n, _):
-        cols = pl.ds(pl.multiple_of(256 * n, 256), 256)
-        res = mm(ht[c], zb[:, :, cols].reshape(2048, 256))
+        cols = pl.ds(pl.multiple_of(512 * n, 512), 512)
+        res = mm(ht[c], zb[:, :, cols].reshape(2048, 512))
         diff = ht[0, :, cols].astype(F32) - ht[1, :, cols].astype(F32)
         lt[:, cols] = (cov * res + (sign * alpha) * diff).astype(BF)
         return 0
 
-    lax.fori_loop(0, 8, factor, 0)
+    lax.fori_loop(0, 4, factor, 0)
 
     theirs = pl.ds(pl.multiple_of(256 * (1 - c), 256), 256)
     ours = pl.ds(pl.multiple_of(256 * c, 256), 256)
 
-    def finish(which, j):
-        def step(p, _):
-            cols = pl.ds(pl.multiple_of(512 * j + 256 * p, 256), 256)
-            at = pl.ds(pl.multiple_of(256 * p, 256), 256)
-            acc[j, which, at] += mm(lt[which, :], cb[:, :, cols].reshape(2048, 256))
-            return 0
-
-        lax.fori_loop(0, 2, step, 0)
-
-    give = []
-    for j in range(4):
-        finish(theirs, j)
-        give.append(go(acc.at[j, theirs, :], orecv.at[j], partner))
-    stores = []
-    for j in range(4):
-        finish(ours, j)
-        give[j].wait_recv()
-        orecv[j] += acc[j, ours, :]
-        stores.append(load(orecv.at[j], out.at[:, pl.ds(512 * j, 512)], 7 + j))
-        stores[j].start()
+    spots = ((0, 0, 512), (1, 0, 512), (2, 0, 512), (3, 0, 256), (3, 256, 256))
+    give, stores = [], []
+
+    for n, (j, low, wide) in enumerate(spots):
+        at = pl.ds(low, wide)
+        where = pl.ds(512 * j + low, wide)
+        right = cb[:, :, 512 * j + low:512 * j + low + wide].reshape(2048, wide)
+        acc[j, :, at] += mm(lt[...], right)
+        give.append(go(acc.at[j, theirs, at], out.at[:, where], partner))
+        stores.append(load(acc.at[j, ours, at], kept.at[:, where], 8 + n))
+        stores[n].start()
+    for copy in give:
+        copy.wait_recv()
     for copy in started:
         copy.wait_send()
     for copy in stores:
@@ -461,27 +460,29 @@
 def body(hidden_a, hidden_b, weight):
     anywhere = pl.BlockSpec(memory_space=pl.ANY)
     vm = pltpu.VMEM
-    return pl.pallas_call(
+    kept, given = pl.pallas_call(
         kernel,
-        out_shape=jax.ShapeDtypeStruct((256, 2048), F32),
+        out_shape=[jax.ShapeDtypeStruct((256, 2048), F32)] * 2,
         in_specs=[anywhere] * 3,
-        out_specs=anywhere,
+        out_specs=[anywhere] * 2,
         scratch_shapes=[
-            vm((2, 512, 1024), BF), vm((2, 1024, 2048), BF), vm((4, 512, 512), F32),
+            vm((2, 512, 1024), BF), vm((1024, 2048), BF), vm((4, 512, 512), F32),
+            vm((4, 512, 512), BF), vm((4, 512, 512), BF),
             vm((4, 128, 512), BF), vm((4, 128, 512), BF), vm((4, 128, 512), BF),
             vm((4, 128, 512), BF), vm((4, 128, 512), BF), vm((4, 128, 512), BF),
             vm((16, 128, 2048), BF), vm((16, 128, 2048), BF), vm((2, 2, 4, 512, 256), BF),
             vm((2, 512, 2048), BF), vm((4, 1, 2048), F32), vm((4, 1, 2048), F32),
             vm((1, 2048), F32), vm((1, 2048), F32), vm((512, 1), F32),
             vm((128, 1152), F32), vm((128, 1152), BF), vm((4, 32, 1152), BF),
-            vm((4, 4, 128, 1152), BF), vm((512, 2048), BF), vm((4, 256, 512), F32),
+            vm((4, 4, 128, 1152), BF), vm((512, 2048), BF),
             pltpu.SemaphoreType.DMA((NSEM,)), pltpu.SemaphoreType.DMA((NSEM,)),
-            pltpu.SemaphoreType.DMA((12,)),
+            pltpu.SemaphoreType.DMA((16,)),
         ],
         compiler_params=pltpu.CompilerParams(
-            collective_id=0, has_side_effects=True, vmem_limit_bytes=67000000),
+            collective_id=0, has_side_effects=True, vmem_limit_bytes=VMEM),
         name="vicreg_grad",
     )(hidden_a, hidden_b, weight)
+    return kept + given
 
 
 def solution(mesh):

time: 143 us -> 129 us (0.902)
  Pallas kernels: 138 us -> 125 us
  other arithmetic: 0 us -> 3.88 us
  local copies, waits for them, and re-layouts: 3.14 us -> 0 us
    pallas_call x1, Pallas kernels: 138 us -> 125 us  [body(): pl.pallas_call(kernel, out_shape=[jax.ShapeDtypeStruct((256, 2048), F32)]...]
    add x0 -> x1, other arithmetic: none -> 3.88 us  [body(): return kept + given]
    unnamed x1 -> x0, local copies, waits for them, and re-layouts: 3.14 us -> none
where the time goes in v3:
time: 129 us
  Pallas kernels  125 us (97%)
  other arithmetic  3.88 us (3%)
    pallas_call x1, Pallas kernels, body(): pl.pallas_call(kernel, out_shape=[jax.ShapeDtypeStruct((256, 2048), F32)]...  125 us
    add x1, other arithmetic, body(): return kept + given  3.88 us

profile of v3, /device:TPU:1, one launch (start us, length us, event | category | flops | bytes accessed | tf_op | source)
XLA Modules:
  0.0 128.9 jit_solution(12517862391499699162)
XLA Ops:
  0.0 125.0 %vicreg_grad.1 = (f32[256,2048]{1,0:T(8,128)}, f32[256,2048]{1,0:T(8,128)}) custom-call(bf16[512,1024]{1,0:T(8,128)(2,1)} %ha.1, bf16[512,1024]{1,0:T(8,128)(2,1)} %hb.1, bf16[1024,2048]{1,0:T(8,128)(2,1)} %w.1), custom_call_target="tpu_custom_call" | custom-call | tf_op jit(solution)/shard_map/vicreg_grad/pallas_call | solution.py:463
  125.0 3.9 %add.3 = f32[256,2048]{1,0:T(8,128)} add(f32[256,2048]{1,0:T(8,128)} %get-tuple-element.7, f32[256,2048]{1,0:T(8,128)} %get-tuple-element.8) | non-fusion elementwise | flops 524288 | bytes 6291456 | tf_op jit(solution)/shard_map/add | solution.py:485

commit v4 on v3

--- a/solution.py
+++ b/solution.py
@@ -126,22 +126,27 @@
         for v, h in enumerate((ha, hb)):
             deal.append((k, v, go(h.at[quarter(t), pl.ds(256 * turn(y, k), 256)], hall.at[v, c, y, quarter(t)], at_y(k))))
 
-    for j in (1, 2, 3):
-        if j < 3:
-            theirs_of(j + 1)
-            give_part(j + 1)
-        ours_of(j)
-        join(j)
+    ours_of(1)
+    join(1)
 
     def send_raw(j):
         raw[j] = go(s_raw.at[j], r_raw.at[j], at_x(-way(j)))
 
     send_raw(0)
     send_raw(1)
-    for j in range(4):
-        relay(j)
+    for j in (2, 3):
+        theirs_of(j)
+        give_part(j)
+    for j in (2, 3):
+        ours_of(j)
+    relay(0)
+    relay(1)
+    join(2)
+    join(3)
     send_raw(2)
     send_raw(3)
+    relay(2)
+    relay(3)
 
     block = 4 * y + x
 
@@ -248,20 +253,16 @@
         for k in ks:
             center(ring.index(k), ring.colour)
 
+    x_rings[0].take()
+    y_rings[0].take()
     center(block, 0)
     center(block, 1)
     center_ring(y_first, (-1, 1))
     center_ring(x_first, (-1, 1))
-    x_rings[0].take()
-    y_rings[0].take()
     y_first.end()
     x_rings[2] = Ring(0, 0, 2)
     x_first.end()
     y_rings[2] = Ring(1, 1, 2)
-    center_ring(y_first, (2,))
-    center_ring(x_first, (2,))
-    center_ring(x_rings[0], (-1, 1))
-    center_ring(y_rings[0], (-1, 1))
 
     def flip(i, _):
         v, r = lax.div(i, 16), lax.rem(i, 16)
@@ -272,35 +273,40 @@
         ht[v, pl.ds(pl.multiple_of(256 * k, 256), 256), pl.ds(where, 256)] = tile.T
         return 0
 
-    for k in (-1, 1, 2):
+    def add_up(i, _):
+        at = pl.ds(pl.multiple_of(128 * i, 128), 128)
+        diff = ht[0, at, :].astype(F32) - ht[1, at, :].astype(F32)
+        dsum[at, :] = jnp.sum(diff, axis=1, keepdims=True)
+        return 0
+
+    center_ring(y_first, (2,))
+    center_ring(x_first, (2,))
+    center_ring(x_rings[0], (-1, 1))
+    center_ring(y_rings[0], (-1, 1))
+    for k in (-1, 1):
         x_rings[k].take()
         y_rings[k].take()
-        before_ring = {-1: 0, 1: -1, 2: 1}[k]
-        x_rings[before_ring].end()
-        y_rings[before_ring].end()
-        center_ring(x_rings[before_ring], (2,))
-        center_ring(y_rings[before_ring], (2,))
+    for copy in handed:
+        copy.wait_recv()
+    lax.fori_loop(0, 16, flip, 0)
+    x_rings[0].end()
+    y_rings[0].end()
+    center_ring(x_rings[0], (2,))
+    center_ring(y_rings[0], (2,))
+    x_rings[2].take()
+    y_rings[2].take()
+    for k in (-1, 1):
         center_ring(x_rings[k], (-1, 1))
         center_ring(y_rings[k], (-1, 1))
-        if k == -1:
-            for copy in handed:
-                copy.wait_recv()
-            lax.fori_loop(0, 16, flip, 0)
-        if k == 1:
-            lax.fori_loop(16, 32, flip, 0)
-        if k == 2:
-
-            def add_up(i, _):
-                part = pl.ds(pl.multiple_of(128 * i, 128), 128)
-                diff = ht[0, part, :].astype(F32) - ht[1, part, :].astype(F32)
-                dsum[part, :] = jnp.sum(diff, axis=1, keepdims=True)
-                return 0
-
-            lax.fori_loop(0, 4, add_up, 0)
-    x_rings[2].end()
-    y_rings[2].end()
-    center_ring(x_rings[2], (2,))
-    center_ring(y_rings[2], (2,))
+    lax.fori_loop(16, 32, flip, 0)
+    lax.fori_loop(0, 4, add_up, 0)
+    center_ring(x_rings[2], (-1, 1))
+    center_ring(y_rings[2], (-1, 1))
+    for k in (-1, 1, 2):
+        x_rings[k].end()
+        center_ring(x_rings[k], (2,))
+        y_rings[k].end()
+        center_ring(y_rings[k], (2,))
 
     mine = cb[block]
 
@@ -308,13 +314,17 @@
         return pl.ds(pl.multiple_of(32 * v, 32), 32)
 
     sums = []
-    for i in range(3):
-        cols = pl.ds(384 * i, 384)
-        right = jnp.concatenate([cb[lax.rem(block + 3 * i + q, 16)] for q in range(3)], axis=0)
+    for p, i in enumerate((None, 0, 1, None, 2)):
+        wide = 256 if p < 4 else 128
+        right = cb[lax.rem(block + 2 * p, 16)]
+        if p < 4:
+            right = jnp.concatenate([right, cb[lax.rem(block + 2 * p + 1, 16)]], axis=0)
         res = mm(mine, right, (((1,), (1,)), ((), ())))
-        gf[:, cols] = res
-        gb[:, cols] = res.astype(BF)
-        sums.append([go(gb.at[strip(turn(t, k)), cols], gr.at[t, :, cols], at_t(k)) for k in (1, 3, 2)])
+        gf[:, 256 * p:256 * p + wide] = res
+        gb[:, 256 * p:256 * p + wide] = res.astype(BF)
+        if i is not None:
+            cols = pl.ds(384 * i, 384)
+            sums.append([go(gb.at[strip(turn(t, k)), cols], gr.at[t, :, cols], at_t(k)) for k in (1, 3, 2)])
 
     class Turn:
         def __init__(self, axis, colour, done, fixed=None, offset=0):
@@ -392,21 +402,18 @@
             one.end()
 
     thirds = {0: third(0)}
-    lax.fori_loop(2, 4, plain, 0)
+    lax.fori_loop(2, 5, plain, 0)
     take(seconds)
     thirds[-1] = third(-1)
     thirds[1] = third(1)
     take(thirds[0])
-    lax.fori_loop(4, 6, plain, 0)
     end(seconds)
     thirds[2] = third(2)
-    lax.fori_loop(6, 7, plain, 0)
+    lax.fori_loop(5, 8, plain, 0)
     take(thirds[-1])
-    end(thirds[0])
     take(thirds[1])
-    lax.fori_loop(7, 8, plain, 0)
     take(thirds[2])
-    for offset in (-1, 1, 2):
+    for offset in (0, -1, 1, 2):
         end(thirds[offset])
 
     for copy in started:

time: 129 us -> 127 us (0.984)
  Pallas kernels: 125 us -> 123 us
    pallas_call x1, Pallas kernels: 125 us -> 123 us  [body(): pl.pallas_call(kernel, out_shape=[jax.ShapeDtypeStruct((256, 2048), F32)]...]
where the time goes in v4:
time: 127 us
  Pallas kernels  123 us (97%)
  other arithmetic  3.88 us (3%)
    pallas_call x1, Pallas kernels, body(): pl.pallas_call(kernel, out_shape=[jax.ShapeDtypeStruct((256, 2048), F32)]...  123 us
    add x1, other arithmetic, body(): return kept + given  3.88 us

profile of v4, /device:TPU:1, one launch (start us, length us, event | category | flops | bytes accessed | tf_op | source)
XLA Modules:
  0.0 127.1 jit_solution(17511903309815687109)
XLA Ops:
  0.0 123.2 %vicreg_grad.1 = (f32[256,2048]{1,0:T(8,128)}, f32[256,2048]{1,0:T(8,128)}) custom-call(bf16[512,1024]{1,0:T(8,128)(2,1)} %ha.1, bf16[512,1024]{1,0:T(8,128)(2,1)} %hb.1, bf16[1024,2048]{1,0:T(8,128)(2,1)} %w.1), custom_call_target="tpu_custom_call" | custom-call | tf_op jit(solution)/shard_map/vicreg_grad/pallas_call | solution.py:470
  123.3 3.9 %add.3 = f32[256,2048]{1,0:T(8,128)} add(f32[256,2048]{1,0:T(8,128)} %get-tuple-element.7, f32[256,2048]{1,0:T(8,128)} %get-tuple-element.8) | non-fusion elementwise | flops 524288 | bytes 6291456 | tf_op jit(solution)/shard_map/add | solution.py:492

commit v5 on v4

--- a/solution.py
+++ b/solution.py
@@ -313,6 +313,8 @@
     def strip(v):
         return pl.ds(pl.multiple_of(32 * v, 32), 32)
 
+    early = list(started)
+    started.clear()
     sums = []
     for p, i in enumerate((None, 0, 1, None, 2)):
         wide = 256 if p < 4 else 128
@@ -413,25 +415,44 @@
     take(thirds[-1])
     take(thirds[1])
     take(thirds[2])
-    for offset in (0, -1, 1, 2):
-        end(thirds[offset])
-
-    for copy in started:
+    for offset in (0, -1, 1):
+        thirds[offset][0].end()
+    for copy in early:
         copy.wait_send()
-    started.clear()
-
-    def spread_panel(b, _):
-        by, bx = lax.div(b, 4), lax.rem(b, 4)
+
+    def put(by, bx, js):
+        b = 4 * by + bx
         here = pl.ds(pl.multiple_of(128 * b, 128), 128)
-        for j in range(9):
+        for j in js:
             other = lax.rem(b + j, 16)
             tile = gp[by, bx, :, 128 * j:128 * j + 128]
             zb[b, :, pl.ds(pl.multiple_of(128 * other, 128), 128)] = tile
             if 0 < j < 8:
                 zb[other, :, here] = tile.T
-        return 0
-
-    lax.fori_loop(0, 16, spread_panel, 0)
+
+    def put_early(i, _):
+        put(lax.rem(y + 3 + lax.div(i, 4), 4), lax.rem(i, 4), range(3))
+        return 0
+
+    lax.fori_loop(0, 12, put_early, 0)
+    for offset in (0, -1, 1):
+        end(thirds[offset][1:])
+    end(thirds[2])
+
+    for copy in started:
+        copy.wait_send()
+    started.clear()
+
+    def put_last(i, _):
+        put(turn(y, 2), i, range(3))
+        return 0
+
+    def put_rest(b, _):
+        put(lax.div(b, 4), lax.rem(b, 4), range(3, 9))
+        return 0
+
+    lax.fori_loop(0, 4, put_last, 0)
+    lax.fori_loop(0, 16, put_rest, 0)
 
     def factor(n, _):
         cols = pl.ds(pl.multiple_of(512 * n, 512), 512)

time: 127 us -> 127 us (level)
  no operation moved by 1% of the time
where the time goes in v5:
time: 127 us
  Pallas kernels  123 us (97%)
  other arithmetic  3.88 us (3%)
    pallas_call x1, Pallas kernels, body(): pl.pallas_call(kernel, out_shape=[jax.ShapeDtypeStruct((256, 2048), F32)]...  123 us
    add x1, other arithmetic, body(): return kept + given  3.88 us

profile of v5, /device:TPU:1, one launch (start us, length us, event | category | flops | bytes accessed | tf_op | source)
XLA Modules:
  0.0 126.8 jit_solution(444438052351867161)
XLA Ops:
  0.0 122.9 %vicreg_grad.1 = (f32[256,2048]{1,0:T(8,128)}, f32[256,2048]{1,0:T(8,128)}) custom-call(bf16[512,1024]{1,0:T(8,128)(2,1)} %ha.1, bf16[512,1024]{1,0:T(8,128)(2,1)} %hb.1, bf16[1024,2048]{1,0:T(8,128)(2,1)} %w.1), custom_call_target="tpu_custom_call" | custom-call | tf_op jit(solution)/shard_map/vicreg_grad/pallas_call | solution.py:491
  122.9 3.9 %add.3 = f32[256,2048]{1,0:T(8,128)} add(f32[256,2048]{1,0:T(8,128)} %get-tuple-element.7, f32[256,2048]{1,0:T(8,128)} %get-tuple-element.8) | non-fusion elementwise | flops 524288 | bytes 6291456 | tf_op jit(solution)/shard_map/add | solution.py:513
